TPU v7x, 32 devices: a whole 2x2x4 slice. The times are simulated.
32 devices in a mesh: mem: 4 (over x, core), lat: 8 (over z, y).
Axes of the slice: x: 2, y: 2, z: 4, core: 2. Of those that a mesh axis runs over, the one named last changes fastest.
Arguments:
- control: bfloat16 [8, 10, 704, 1440], P('mem', None, 'lat'), may hold values from -6 to 6
- perturb: bfloat16 [8, 10, 704, 1440], P('mem', None, None, 'lat'), may hold values from -6 to 6
- lon_loc: bfloat16 [1440, 1440], P(None, 'mem'), may hold values from 0 to 1, as said below
- lat_loc: bfloat16 [704, 704], P('mem'), may hold values from 0 to 1, as said below
- static_scale: float32 [10, 704, 1440], P(None, 'mem', 'lat'), may hold values from 0.3 to 1
- static_field: float32 [10, 704, 1440], P(None, 'mem', 'lat'), may hold values from -6 to 6
- courant: float32 [2, 704, 1440], P(None, 'mem', 'lat'), may hold values from -0.48 to 0.48
Outputs:
- increment: float32 [10, 704, 1440], P(None, 'mem', 'lat')
- evolved: float32 [10, 704, 1440], P(None, 'mem', 'lat')
Inputs may be any that keep to these rules, and one draw needn't show every extreme that they name: `lon_loc`: Symmetric, with positive entries. `lat_loc`: Symmetric, with positive entries.
All inputs are finite; a program needn't handle non-finite values.
Results may differ from a plain program's by a relative error of at most 0.0027.
Values may be sent and summed in bfloat16 or wider, within the bound.
No kernel may reach another device: no remote copies, remote signals or barrier semaphores. Data moves between devices by JAX's collectives and lax.ppermute only.
A program may use at most 128 MiB of HBM per device.

v0:
```python
import math
import jax
import jax.numpy as jnp
from jax import lax
from jax.sharding import PartitionSpec as P

NLAT = 704
STEPS = 4


def padded_2(shard, sides, width, wrap):
    for axis, dim in sides:
        size, length = (lax.axis_size(axis), shard.shape[dim])
        up = [(i, (i + 1) % size) for i in range(size if wrap else size - 1)]
        down = [(j, i) for i, j in up]
        last = lax.slice_in_dim(shard, length - width, length, axis=dim)
        leading = lax.slice_in_dim(shard, 0, width, axis=dim)
        before = lax.ppermute(last, axis, up)
        after = lax.ppermute(leading, axis, down)
        shard = jnp.concatenate([before, shard, after], axis=dim)
    return shard


def upwind(padded, east_west, north_south):
    center = padded[:, 1:-1, 1:-1]
    western = padded[:, 1:-1, :-2]
    eastern = padded[:, 1:-1, 2:]
    southern = padded[:, :-2, 1:-1]
    northern = padded[:, 2:, 1:-1]
    zonal = jnp.maximum(east_west, 0.0) * (center - western) + jnp.minimum(east_west, 0.0) * (
        eastern - center
    )
    meridional = jnp.maximum(north_south, 0.0) * (center - southern) + jnp.minimum(
        north_south, 0.0
    ) * (northern - center)
    return center - zonal - meridional


def lon_rim(values, width):
    return padded_2(values, (("lat", 2),), width, True)


def lat_rim(values, width):
    return padded_2(values, (("mem", 1),), width, False)


def evolve(current, courant):
    fields = current.shape[0]
    stacked = jnp.concatenate([current, courant], axis=0)
    extended = lat_rim(lon_rim(stacked, STEPS), STEPS)
    result = extended[:fields]
    wind_ext = extended[fields:]
    for step_index in range(STEPS):
        margin = step_index + 1
        inner_wind = wind_ext[
            :, margin : wind_ext.shape[1] - margin, margin : wind_ext.shape[2] - margin
        ]
        result = upwind(result, inner_wind[0], inner_wind[1])
    return result


def per_device(control, perturb, lon_loc, lat_loc, static_scale, static_field, courant):
    along_lon = jnp.einsum(
        "mfal,lc->amfc",
        control,
        lax.all_gather(lon_loc, "mem", axis=1, tiled=True),
        preferred_element_type=jnp.float32,
    ).astype(jnp.bfloat16)
    banded = lax.all_to_all(along_lon, "lat", split_axis=3, concat_axis=0, tiled=True)
    mem_here = banded.shape[1]
    fields = banded.shape[2]
    lon_width = banded.shape[3]
    flat_band = banded.reshape(banded.shape[0], mem_here * fields * lon_width)
    pert_rows = jnp.transpose(perturb, (2, 0, 1, 3))
    lat_weights_all = lax.all_gather(lat_loc, "mem", axis=0, tiled=True)
    members = mem_here * lax.axis_size("mem")
    ens_scale = 1.0 / math.sqrt(members - 1)
    rows_own = NLAT // lax.axis_size("mem")
    localized = jnp.dot(lat_weights_all, flat_band, preferred_element_type=jnp.float32)
    localized = localized.reshape(NLAT, mem_here, fields, lon_width)
    ensemble_all = jnp.transpose(
        lax.psum(jnp.sum(localized * pert_rows.astype(jnp.float32), axis=1) * ens_scale, "mem"),
        (1, 0, 2),
    )
    offset = lax.axis_index("mem") * rows_own
    ensemble = lax.dynamic_slice_in_dim(ensemble_all, offset, rows_own, 1)
    increment = ensemble + static_scale * static_field
    evolved = evolve(increment, courant)
    return (increment, evolved)


def solution(mesh):
    placed = (
        P("mem", None, "lat", None),
        P("mem", None, None, "lat"),
        P(None, "mem"),
        P("mem", None),
        P(None, "mem", "lat"),
        P(None, "mem", "lat"),
        P(None, "mem", "lat"),
    )
    return jax.shard_map(
        per_device,
        mesh=mesh,
        in_specs=placed,
        out_specs=(P(None, "mem", "lat"), P(None, "mem", "lat")),
        check_vma=False,
    )
```

profile of v0, /device:TPU:1, one launch (start us, length us, event | category | flops | bytes accessed | tf_op | source)
XLA Modules:
  0.0 472.6 jit_solution(8537434043374464706)
XLA Ops:
  7.2 2.4 copy.32
  9.6 38.8 %all-gather.2.cloned.1.call-done = bf16[1440,1440]{0,1:T(8,128)(2,1)} async-done(((bf16[1440,360]{0,1:T(8,128)(2,1)}), bf16[1440,1440]{0,1:T(8,128)(2,1)}) %all-gather.2.cloned.1.call-update) | async-done | bytes 4147216 | tf_op jit(solution)/shard_map/all_gather | solution.py:66
  48.4 13.5 %convert_bitcast_fusion = bf16[88,2,10,1440]{3,0,2,1:T(8,128)(2,1)} fusion(bf16[2,10,88,1440]{3,2,1,0:T(8,128)(2,1)} %param.7, bf16[1440,1440]{0,1:T(8,128)(2,1)} %all-gather.2.cloned.1.call-done), kind=kOutput, calls=%fused_computation.4 | convolution fusion | flops 7301606400 | bytes 14284800 | tf_op jit(solution)/shard_map/mfal,lc->amfc/dot_general | solution.py:63
  61.8 16.8 %copy.34 = bf16[88,2,10,1440]{0,1,2,3:T(2,128)(2,1)} copy(bf16[88,2,10,1440]{3,0,2,1:T(8,128)(2,1)} %convert_bitcast_fusion) | data formatting | bytes 10137600 | tf_op jit(solution)/shard_map/convert_element_type | solution.py:68
  78.6 5.4 %all-to-all-start = ((bf16[88,2,10,1440]{0,1,2,3:T(2,128)(2,1)}), bf16[88,2,10,1440]{0,1,2,3:T(2,128)(2,1)}, u32[]{:S(2)}, u32[]{:S(2)}) async-start(bf16[88,2,10,1440]{0,1,2,3:T(2,128)(2,1)} %copy.34), calls=%async_computation | async-start | bytes 14745600 | tf_op jit(solution)/shard_map/all_to_all | solution.py:69
  84.0 10.5 %all_gather.7 = bf16[704,704]{1,0:T(8,128)(2,1)S(1)} all-gather(bf16[176,704]{1,0:T(8,128)(2,1)S(1)} %copy-done.7), channel_id=1, replica_groups=mesh['mem'=4,'lat'=8] {'mem'}, dimensions={0}, use_global_device_ids=true | all-gather | bytes 1239040 | tf_op jit(solution)/shard_map/all_gather | solution.py:75
  94.5 150.4 %all-to-all-done = bf16[88,2,10,1440]{0,1,2,3:T(2,128)(2,1)} async-done(((bf16[88,2,10,1440]{0,1,2,3:T(2,128)(2,1)}), bf16[88,2,10,1440]{0,1,2,3:T(2,128)(2,1)}, u32[]{:S(2)}, u32[]{:S(2)}) %all-to-all-start) | async-done | bytes 5068832 | tf_op jit(solution)/shard_map/all_to_all | solution.py:69
  245.0 8.0 %copy.59 = bf16[88,2,10,8,180]{0,3,4,2,1:T(8,128)(2,1)} copy(bf16[88,2,10,8,180]{0,1,2,4,3:T(2,128)(2,1)} %bitcast.2) | data formatting | bytes 10137600 | tf_op jit(solution)/shard_map/all_to_all | solution.py:69
  253.0 12.2 %reshape.11 = bf16[704,3600]{0,1:T(8,128)(2,1)} reshape(bf16[8,88,2,10,180]{1,0,4,3,2:T(8,128)(2,1)} %bitcast.58) | data formatting | bytes 10137600 | tf_op jit(solution)/shard_map/reshape | solution.py:73
  265.2 9.6 %convolution_bitcast_fusion = f32[704,3600]{1,0:T(8,128)} fusion(bf16[704,3600]{0,1:T(8,128)(2,1)} %reshape.11, bf16[704,704]{1,0:T(8,128)(2,1)S(1)} %all_gather.7), kind=kOutput, calls=%fused_computation.3 | convolution fusion | flops 3568435200 | bytes 16197632 | tf_op jit(solution)/shard_map/dot_general | solution.py:79
  274.7 11.8 %copy.36 = f32[704,3600]{0,1:T(8,128)} copy(f32[704,3600]{1,0:T(8,128)} %convolution_bitcast_fusion) | data formatting | bytes 20275200 | tf_op jit(solution)/shard_map/dot_general | solution.py:79
  286.6 11.6 %reshape.12 = f32[704,2,10,180]{0,3,2,1:T(8,128)} reshape(f32[704,3600]{0,1:T(8,128)} %copy.36) | data formatting | bytes 20275200 | tf_op jit(solution)/shard_map/reshape | solution.py:80
  298.1 10.3 %fusion = f32[704,10,180]{0,2,1:T(8,128)} fusion(f32[704,2,10,180]{0,3,2,1:T(8,128)} %reshape.12, bf16[2,10,704,180]{2,0,3,1:T(2,128)(2,1)} %param.8), kind=kLoop, calls=%fused_computation.1 | loop fusion | flops 6336000 | bytes 20275200 | tf_op jit(solution)/shard_map/reduce_sum | solution.py:82
  308.4 5.5 %broadcast_multiply_fusion = f32[704,10,180]{0,2,1:T(8,128)} fusion(f32[704,10,180]{0,2,1:T(8,128)} %fusion), kind=kLoop, calls=%fused_computation.6 | loop fusion | flops 1267200 | bytes 10137600 | tf_op jit(solution)/shard_map/mul | solution.py:82
  317.3 3.0 copy.39
  320.5 101.5 %all-reduce.2.cloned.1.call-done = f32[704,10,180]{0,2,1:T(8,128)} async-done(((f32[704,10,180]{0,2,1:T(8,128)}), f32[704,10,180]{0,2,1:T(8,128)}) %all-reduce.2.cloned.1.call-update) | async-done | bytes 5068816 | tf_op jit(solution)/shard_map/psum | solution.py:82
  422.0 3.5 bitcast_add_fusion
  426.8 3.0 collective-permute-start.1
  433.2 2.4 copy.45
  435.6 4.1 collective-permute-start.2
  440.8 2.1 collective-permute-start.3
  450.3 2.2 copy.48
  455.6 2.1 fusion.4
  461.8 2.1 fusion.12
  (52 shorter events, 25.5 us)
Async XLA Ops:
  7.2 41.2 %all-gather.2.cloned.1.call-start = ((), (), s32[]{:S(2)}) async-start(), calls=%async_computation.1 | async-start | bytes 5529600 | tf_op jit(solution)/shard_map/all_gather | solution.py:66
  78.6 5.4 %copy-start.7 = (bf16[176,704]{1,0:T(8,128)(2,1)S(1)}, bf16[176,704]{1,0:T(8,128)(2,1)}, u32[]{:S(2)}) copy-start(bf16[176,704]{1,0:T(8,128)(2,1)} %param.10) | copy-start | bytes 743428
  78.6 166.4 %all-to-all-start = ((bf16[88,2,10,1440]{0,1,2,3:T(2,128)(2,1)}), bf16[88,2,10,1440]{0,1,2,3:T(2,128)(2,1)}, u32[]{:S(2)}, u32[]{:S(2)}) async-start(bf16[88,2,10,1440]{0,1,2,3:T(2,128)(2,1)} %copy.34), calls=%async_computation | async-start | bytes 14745600 | tf_op jit(solution)/shard_map/all_to_all | solution.py:69
  84.0 338.0 %all-reduce.2.cloned.1.call-start = ((), (), s32[]{:S(2)}) async-start(), calls=%async_computation.2 | async-start | bytes 11304960 | tf_op jit(solution)/shard_map/psum | solution.py:82
  313.9 1.5 copy-start.1
  317.3 3.0 copy-start.2
  425.6 5.9 %collective-permute-start = (f32[12,176,4]{1,0,2:T(8,128)S(1)}, f32[12,176,4]{1,0,2:T(8,128)S(1)}, u32[]{:S(2)}, u32[]{:S(2)}) collective-permute-start(f32[12,176,4]{1,0,2:T(8,128)S(1)} %copy.41), channel_id=1, source_target_pairs={{0,1},{1,2},{2,3},{3,4},{4,5},{5,6},{6,7},{7,0},{8,9},{9,10},{10,1... | collective-permute-start | bytes 101384 | tf_op jit(solution)/shard_map/ppermute | solution.py:18
  426.8 4.7 collective-permute-start.1
  435.6 13.4 %collective-permute-start.2 = (f32[12,4,188]{2,1,0:T(4,128)}, f32[12,4,188]{2,1,0:T(4,128)}, u32[]{:S(2)}, u32[]{:S(2)}) collective-permute-start(f32[12,4,188]{2,1,0:T(4,128)} %copy.45), channel_id=1, source_target_pairs={{0,8},{8,16},{16,24},{1,9},{9,17},{17,25},{2,10},{10,18},{18,26},{... | collective-permute-start | bytes 108296 | tf_op jit(solution)/shard_map/ppermute | solution.py:18
  440.8 9.4 %collective-permute-start.3 = (f32[12,4,188]{2,1,0:T(4,128)}, f32[12,4,188]{2,1,0:T(4,128)}, u32[]{:S(2)}, u32[]{:S(2)}) collective-permute-start(f32[12,4,188]{2,1,0:T(4,128)} %copy.46), channel_id=1, source_target_pairs={{8,0},{16,8},{24,16},{9,1},{17,9},{25,17},{10,2},{18,10},{26,18},{... | collective-permute-start | bytes 108296 | tf_op jit(solution)/shard_map/ppermute | solution.py:19
  452.5 1.4 copy-start
  459.7 2.1 copy-start.3
  459.7 2.1 copy-start.4
  459.7 2.1 copy-start.5
  459.7 2.1 copy-start.6
Sparse Core Ops, SparseCore 0:
  10.1 38.2 all-gather.1
  314.1 107.8 all-reduce.1
where the time goes:
time: 474 us; the launch traced here: 473 us
  waiting for transfers between devices  292 us (62%)
  local copies, waits for them, and re-layouts  84.6 us (18%)
  other arithmetic  31.8 us (7%)
  matrix products  23 us (5%)
  starting transfers between devices  16 us (3%)
  between operations  14.3 us (3%)
  blocking collectives  10.5 us (2%)
    all_to_all x1, waiting for transfers between devices, per_device(): lax.all_to_all(along_lon, 'lat', split_axis=3, concat_axis=0, tiled=True)  150 us
    psum x1, waiting for transfers between devices, per_device(): lax.psum(jnp.sum(localized * pert_rows.astype(jnp.float32), axis=1) * ens...  102 us
    all_gather x1, waiting for transfers between devices, per_device(): lax.all_gather(lon_loc, 'mem', axis=1, tiled=True)  38.8 us
    convert_element_type x1, local copies, waits for them, and re-layouts, per_device(): along_lon = jnp.einsum('mfal,lc->amfc', control, lax.all_gather(lon_loc,...  16.8 us
    dot_general x1, matrix products, per_device(): jnp.einsum('mfal,lc->amfc', control, lax.all_gather(lon_loc, 'mem', axis=...  13.5 us
    unnamed x22, local copies, waits for them, and re-layouts  12.6 us
    reshape x1, local copies, waits for them, and re-layouts, per_device(): flat_band = banded.reshape(banded.shape[0], mem_here * fields * lon_width)  12.2 us
    dot_general x1, local copies, waits for them, and re-layouts, per_device(): jnp.dot(lat_weights_all, flat_band, preferred_element_type=jnp.float32)  11.8 us
  transfers between devices with their start and end apart: 7, of which 4 were waited for; matrix products, arithmetic and copies ran while one was open for 3% of the time, Pallas kernels for 0%

commit v1 on v0

--- a/solution.py
+++ b/solution.py
@@ -79,7 +79,12 @@
     localized = jnp.dot(lat_weights_all, flat_band, preferred_element_type=jnp.float32)
     localized = localized.reshape(NLAT, mem_here, fields, lon_width)
     ensemble_all = jnp.transpose(
-        lax.psum(jnp.sum(localized * pert_rows.astype(jnp.float32), axis=1) * ens_scale, "mem"),
+        jnp.sum(
+            lax.all_gather(
+                jnp.sum(localized * pert_rows.astype(jnp.float32), axis=1) * ens_scale, "mem"
+            ),
+            axis=0,
+        ),
         (1, 0, 2),
     )
     offset = lax.axis_index("mem") * rows_own

time: 474 us -> 705 us (1.49)
  waiting for transfers between devices: 292 us -> 465 us
  other arithmetic: 31.8 us -> 82.6 us
    all_gather x0 -> x1, waiting for transfers between devices: none -> 272 us  [per_device(): lax.all_gather(jnp.sum(localized * pert_rows.astype(jnp.float32), axis=1)...]
    psum x1 -> x0, waiting for transfers between devices: 102 us -> none  [per_device(): lax.psum(jnp.sum(localized * pert_rows.astype(jnp.float32), axis=1) * ens...]
    reduce_sum x0 -> x1, other arithmetic: none -> 34.7 us  [per_device(): jnp.sum(lax.all_gather(jnp.sum(localized * pert_rows.astype(jnp.float32),...]
    mul x4 -> x1, local copies, waits for them, and re-layouts: 3.15 us -> 12.1 us  [per_device(): jnp.sum(localized * pert_rows.astype(jnp.float32), axis=1) * ens_scale]
  transfers between devices with their start and end apart: 7 -> 7, of which waited for: 4 -> 4; matrix products, arithmetic and copies ran while one was open for 3% -> 1% of each run, Pallas kernels for 0% -> 0%
where the time goes in v1:
time: 705 us; the launch traced here: 699 us
  waiting for transfers between devices  465 us (66%)
  local copies, waits for them, and re-layouts  88.4 us (13%)
  other arithmetic  82.6 us (12%)
  matrix products  23 us (3%)
  starting transfers between devices  15.4 us (2%)
  between operations  14.5 us (2%)
  blocking collectives  10.7 us (2%)
    all_gather x1, waiting for transfers between devices, per_device(): lax.all_gather(jnp.sum(localized * pert_rows.astype(jnp.float32), axis=1)...  272 us
    all_to_all x1, waiting for transfers between devices, per_device(): lax.all_to_all(along_lon, 'lat', split_axis=3, concat_axis=0, tiled=True)  150 us
    all_gather x1, waiting for transfers between devices, per_device(): lax.all_gather(lon_loc, 'mem', axis=1, tiled=True)  38.8 us
    reduce_sum x1, other arithmetic, per_device(): jnp.sum(lax.all_gather(jnp.sum(localized * pert_rows.astype(jnp.float32),...  34.7 us
    convert_element_type x1, local copies, waits for them, and re-layouts, per_device(): along_lon = jnp.einsum('mfal,lc->amfc', control, lax.all_gather(lon_loc,...  16.8 us
  transfers between devices with their start and end apart: 7, of which 4 were waited for; matrix products, arithmetic and copies ran while one was open for 1% of the time, Pallas kernels for 0%

profile of v1, /device:TPU:1, one launch (start us, length us, event | category | flops | bytes accessed | tf_op | source)
XLA Modules:
  0.0 699.5 jit_solution(16696181768635476713)
XLA Ops:
  9.6 38.8 %all-gather.4.cloned.1.call-done = bf16[1440,1440]{0,1:T(8,128)(2,1)} async-done(((bf16[1440,360]{0,1:T(8,128)(2,1)}), bf16[1440,1440]{0,1:T(8,128)(2,1)}) %all-gather.4.cloned.1.call-update) | async-done | bytes 4147216 | tf_op jit(solution)/shard_map/all_gather | solution.py:66
  48.4 13.5 %convert_bitcast_fusion = bf16[88,2,10,1440]{3,0,2,1:T(8,128)(2,1)} fusion(bf16[2,10,88,1440]{3,2,1,0:T(8,128)(2,1)} %param.7, bf16[1440,1440]{0,1:T(8,128)(2,1)} %all-gather.4.cloned.1.call-done), kind=kOutput, calls=%fused_computation.4 | convolution fusion | flops 7301606400 | bytes 14284800 | tf_op jit(solution)/shard_map/mfal,lc->amfc/dot_general | solution.py:63
  61.8 16.8 %copy.42 = bf16[88,2,10,1440]{0,1,2,3:T(2,128)(2,1)} copy(bf16[88,2,10,1440]{3,0,2,1:T(8,128)(2,1)} %convert_bitcast_fusion) | data formatting | bytes 10137600 | tf_op jit(solution)/shard_map/convert_element_type | solution.py:68
  78.6 5.4 all-to-all-start
  84.0 10.7 %all_gather.11 = bf16[704,704]{1,0:T(8,128)(2,1)S(1)} all-gather(bf16[176,704]{1,0:T(8,128)(2,1)S(1)} %copy-done.4), channel_id=1, replica_groups=mesh['mem'=4,'lat'=8] {'mem'}, dimensions={0}, use_global_device_ids=true | all-gather | bytes 1239040 | tf_op jit(solution)/shard_map/all_gather | solution.py:75
  94.7 150.2 %all-to-all-done = bf16[88,2,10,1440]{0,1,2,3:T(2,128)(2,1)} async-done(((bf16[88,2,10,1440]{0,1,2,3:T(2,128)(2,1)}), bf16[88,2,10,1440]{0,1,2,3:T(2,128)(2,1)}, u32[]{:S(2)}, u32[]{:S(2)}) %all-to-all-start) | async-done | bytes 5068832 | tf_op jit(solution)/shard_map/all_to_all | solution.py:69
  245.0 8.0 %copy.88 = bf16[88,2,10,8,180]{0,3,4,2,1:T(8,128)(2,1)} copy(bf16[88,2,10,8,180]{0,1,2,4,3:T(2,128)(2,1)} %bitcast.2) | data formatting | bytes 10137600 | tf_op jit(solution)/shard_map/all_to_all | solution.py:69
  253.0 12.2 %reshape.20 = bf16[704,3600]{0,1:T(8,128)(2,1)} reshape(bf16[8,88,2,10,180]{1,0,4,3,2:T(8,128)(2,1)} %bitcast.66) | data formatting | bytes 10137600 | tf_op jit(solution)/shard_map/reshape | solution.py:73
  265.2 9.5 %convolution_bitcast_fusion = f32[704,3600]{1,0:T(8,128)} fusion(bf16[704,3600]{0,1:T(8,128)(2,1)} %reshape.20, bf16[704,704]{1,0:T(8,128)(2,1)S(1)} %all_gather.11), kind=kOutput, calls=%fused_computation.3 | convolution fusion | flops 3568435200 | bytes 16197632 | tf_op jit(solution)/shard_map/dot_general | solution.py:79
  274.7 11.8 %copy.44 = f32[704,3600]{0,1:T(8,128)} copy(f32[704,3600]{1,0:T(8,128)} %convolution_bitcast_fusion) | data formatting | bytes 20275200 | tf_op jit(solution)/shard_map/dot_general | solution.py:79
  286.6 11.6 %reshape.21 = f32[704,2,10,180]{0,3,2,1:T(8,128)} reshape(f32[704,3600]{0,1:T(8,128)} %copy.44) | data formatting | bytes 20275200 | tf_op jit(solution)/shard_map/reshape | solution.py:80
  298.1 10.3 %fusion = f32[704,10,180]{0,2,1:T(8,128)} fusion(f32[704,2,10,180]{0,3,2,1:T(8,128)} %reshape.21, bf16[2,10,704,180]{2,0,3,1:T(2,128)(2,1)} %param.8), kind=kLoop, calls=%fused_computation.1 | loop fusion | flops 6336000 | bytes 20275200 | tf_op jit(solution)/shard_map/reduce_sum | solution.py:84
  308.4 5.5 broadcast_multiply_fusion
  313.9 12.1 %copy.46 = f32[704,10,180]{2,1,0:T(8,128)} copy(f32[704,10,180]{0,2,1:T(8,128)} %broadcast_multiply_fusion) | data formatting | bytes 10137600 | tf_op jit(solution)/shard_map/mul | solution.py:84
  327.3 271.7 %all-gather.6.cloned.1.call-done = f32[2816,10,180]{2,1,0:T(8,128)} async-done(((f32[704,10,180]{2,1,0:T(8,128)}), f32[2816,10,180]{2,1,0:T(8,128)}) %all-gather.6.cloned.1.call-update) | async-done | bytes 20275216 | tf_op jit(solution)/shard_map/all_gather | solution.py:83
  599.0 34.7 %reduce_sum.19 = f32[704,10,180]{2,1,0:T(8,128)} reduce(f32[4,704,10,180]{3,2,1,0:T(8,128)} %bitcast.65, f32[]{:T(128)} %constant.6.clone.1), dimensions={0}, to_apply=%region_1.0 | reduce | flops 3801600 | bytes 25344004 | tf_op jit(solution)/shard_map/reduce_sum | solution.py:82
  633.7 5.1 bitcast_add_fusion
  643.0 4.0 collective-permute-start.1
  650.8 4.0 collective-permute-done
  657.6 3.9 collective-permute-start.3
  676.0 3.7 fusion.4
  679.7 3.5 fusion.12
  683.3 3.5 fusion.20
  686.8 3.3 fusion.28
  (46 shorter events, 31.2 us)
Async XLA Ops:
  7.2 41.2 %all-gather.4.cloned.1.call-start = ((), (), s32[]{:S(2)}) async-start(), calls=%async_computation.1 | async-start | bytes 5529600 | tf_op jit(solution)/shard_map/all_gather | solution.py:66
  78.6 5.4 copy-start.4
  78.6 166.4 %all-to-all-start = ((bf16[88,2,10,1440]{0,1,2,3:T(2,128)(2,1)}), bf16[88,2,10,1440]{0,1,2,3:T(2,128)(2,1)}, u32[]{:S(2)}, u32[]{:S(2)}) async-start(bf16[88,2,10,1440]{0,1,2,3:T(2,128)(2,1)} %copy.42), calls=%async_computation | async-start | bytes 14745600 | tf_op jit(solution)/shard_map/all_to_all | solution.py:69
  84.0 515.1 %all-gather.6.cloned.1.call-start = ((), (), s32[]{:S(2)}) async-start(), calls=%async_computation.2 | async-start | bytes 57671680 | tf_op jit(solution)/shard_map/all_gather | solution.py:83
  326.0 1.0 copy-start.2
  643.0 6.1 collective-permute-start.1
  649.0 5.9 collective-permute-start
  656.6 7.0 copy-start.3
  657.6 8.3 %copy-start = (f32[12,176,4]{2,0,1:T(8,128)S(1)}, f32[12,176,4]{2,0,1:T(8,128)}, u32[]{:S(2)}) copy-start(f32[12,176,4]{2,0,1:T(8,128)} %copy.53) | copy-start | bytes 101380
  657.6 8.3 %copy-start.1 = (f32[12,176,4]{2,0,1:T(8,128)S(1)}, f32[12,176,4]{2,0,1:T(8,128)}, u32[]{:S(2)}) copy-start(f32[12,176,4]{2,0,1:T(8,128)} %copy.52) | copy-start | bytes 101380
  657.6 8.3 %collective-permute-start.3 = (f32[12,4,188]{2,0,1:T(8,128)S(1)}, f32[12,4,188]{2,0,1:T(8,128)S(1)}, u32[]{:S(2)}, u32[]{:S(2)}) collective-permute-start(f32[12,4,188]{2,0,1:T(8,128)S(1)} %get-tuple-element.25), channel_id=1, source_target_pairs={{8,0},{16,8},{24,16},{9,1},{17,9},{25,17},{10,2},{18,10},{26,18},{... | collective-permute-start | bytes 108296 | tf_op jit(solution)/shard_map/ppermute | solution.py:19
  661.5 4.4 collective-permute-start.2
Sparse Core Ops, SparseCore 0:
  10.1 38.2 all-gather.3
  326.2 272.7 all-gather.5
